TPU v7x, 512 devices: a whole 4x4x16 slice. The times are simulated.
512 devices in a mesh: row: 8 (over z_hi, core), col: 16 (over y, z_lo), dp: 4 (over x).
Axes of the slice: x: 4, y: 4, z: 16 (z_hi: 4, z_lo: 4; z = z_hi * 4 + z_lo), core: 2. Of those that a mesh axis runs over, the one named last changes fastest.
Arguments:
- activations: bfloat16 [4, 1024, 16384], P('dp', 'col', 'row'), may hold values from -6 to 6
- out_grads: bfloat16 [4, 1024, 4096], P('dp', 'row', 'col'), may hold values from -6 to 6
- block_mask: int32 [128, 32], P('row', 'col'), may hold values from 0 to 1, as said below
- master_weight: float32 [16384, 4096], P(('row', 'dp'), 'col'), may hold values from -0.046875 to 0.046875
- first_moment: float32 [16384, 4096], P(('row', 'dp'), 'col'), may hold values from -12 to 12
- second_moment: float32 [16384, 4096], P(('row', 'dp'), 'col'), may hold values from 0.05 to 2
Outputs:
- input_grads: bfloat16 [4, 1024, 16384], P('dp', 'col', 'row')
- new_weight: float32 [16384, 4096], P(('row', 'dp'), 'col')
- new_first: float32 [16384, 4096], P(('row', 'dp'), 'col')
- new_second: float32 [16384, 4096], P(('row', 'dp'), 'col')
Inputs may be any that keep to these rules, and one draw needn't show every extreme that they name: `block_mask`: 1 where the 128 x 128 block of the weight is kept, 0 where it is pruned.
All inputs are finite; a program needn't handle non-finite values.
Results may differ from a plain program's by a relative error of at most 0.015.
Values may be sent and summed in bfloat16 or wider, within the bound.
No kernel may reach another device: no remote copies, remote signals or barrier semaphores. Data moves between devices by JAX's collectives and lax.ppermute only.
A program may use at most 64 MiB of HBM per device.

v0:
```python
import jax
import jax.numpy as jnp
from jax import lax
from jax.experimental import pallas as pl
from jax.experimental.pallas import tpu as pltpu
from jax.sharding import Mesh
from jax.sharding import PartitionSpec as P

BLOCK = 128
ROW = ("zh", "core")
COL = ("y", "zl")
ROW_X = ("zh", "core", "x")


first_decay = 0.9
second_decay = 0.999
learn_rate = 0.001
adam_epsilon = 1e-08
first_correct = 1.0 - 0.9**10
second_correct = 1.0 - 0.999**10


def from_everyone(array, axis):
    copies = jnp.broadcast_to(array, (lax.axis_size(axis), *array.shape))
    return lax.all_to_all(copies, axis, split_axis=0, concat_axis=0, tiled=True)


def shifted(array, axis, by):
    peers = lax.axis_size(axis)
    return lax.ppermute(array, axis, [(k, (k + by) % peers) for k in range(peers)])


def partners(index):
    first = index + 1 - 2 * (index % 2)
    return (index, first, 3 - index, 3 - first)


def swapped(array, axis, which):
    return lax.ppermute(array, axis, [(k, partners(k)[which]) for k in range(4)])


def expand(block_keep):
    tall, broad = block_keep.shape
    values = block_keep.astype(jnp.float32)
    grown = jnp.broadcast_to(values[:, None, :, None], (tall, BLOCK, broad, BLOCK))
    return grown.reshape(tall * BLOCK, broad * BLOCK)


def ring_place(index, step):
    return lax.rem(index + 4 - step, 4)


def start_all(copies):
    for copy in copies:
        copy.start()
    return copies


def wait_all(copies):
    for copy in copies:
        copy.wait()


def gather_grads(source, tile, sems, y):
    cols = source.shape[-1]
    return [
        pltpu.make_async_copy(source.at[:, place_y], tile.at[:, :, pl.ds(s * cols, cols)], sems.at[s])
        for s, place_y in enumerate(partners(y))
    ]


def half_inputs(where, place, source, near, far, out, tile, weights, result, sems):
    cols = near.shape[-1]
    copies = [
        pltpu.make_async_copy((near, far)[s // 2].at[s % 2], weights.at[:, pl.ds(s * cols, cols)], sems.at[4 + s])
        for s in range(4)
    ]
    wait_all(start_all(gather_grads(source, tile, sems, place[1]) + copies))
    groups, tokens, deep = tile.shape
    step = groups // 2
    sent = []
    for k in range(2):
        mine = pl.ds(k * step, step)
        part = lax.dot_general(
            tile[mine].reshape(step * tokens, deep),
            weights[...],
            (((1,), (1,)), ((), ())),
            preferred_element_type=jnp.float32,
        ).astype(jnp.bfloat16)
        result[mine] = part.reshape(step, *result.shape[1:])
        sent += start_all([pltpu.make_async_copy(result.at[mine], out.at[mine, where], sems.at[8 + k])])
    wait_all(sent)


def own_half_kernel(place, source, near, far, out, *scratch):
    half_inputs(place[3], place, source, near, far, out, *scratch)


def other_half_kernel(place, source, near, far, begun, out, *scratch):
    half_inputs(1 - place[3], place, source, near, far, out, *scratch)


def weights_kernel(place, mine, theirs, a0, a1, a2, a3, o0, o1, o2, o3, tile, acts, turned, sems):
    x, y, zl, core = place[0], place[1], place[2], place[3]
    copies = []
    for t, piece in enumerate((a0, a1, a2, a3)):
        where = ring_place(zl, t)
        half = lax.rem(where // 2 + core, 2)
        for s, place_x in enumerate(partners(x)):
            copies.append(
                pltpu.make_async_copy(
                    piece.at[s],
                    acts.at[half, place_x, lax.rem(where, 2)],
                    sems.at[8 + t * 4 + s],
                )
            )
    start_all(copies)
    tiles = start_all(
        gather_grads(mine, tile.at[0], sems.at[pl.ds(0, 4)], y)
        + gather_grads(theirs, tile.at[1], sems.at[pl.ds(4, 4)], y)
    )
    wait_all(copies)
    total = tile.shape[0] * tile.shape[1] * tile.shape[2]
    turned[...] = acts[...].reshape(total, acts.shape[-1]).T
    wait_all(tiles)
    cols = o0.shape[-1]
    for s, out in enumerate((o0, o1, o2, o3)):
        right = tile[:, :, :, s * cols : (s + 1) * cols].reshape(total, cols)
        out[...] = lax.dot_general(
            turned[...], right, (((1,), (0,)), ((), ())), preferred_element_type=jnp.float32
        ).astype(jnp.bfloat16)


def sum_kernel(parts, out, held, result, sems):
    blocks, peers, _, wide = held.shape
    copies = start_all([pltpu.make_async_copy(parts.at[k], held.at[k], sems.at[k]) for k in range(blocks)])
    sent = []
    for k in range(blocks):
        copies[k].wait()
        total = held[k, 0].astype(jnp.float32)
        for j in range(1, peers):
            total = total + held[k, j].astype(jnp.float32)
        mine = pl.ds(k * wide, wide)
        result[:, mine] = total.astype(jnp.bfloat16)
        sent += start_all([pltpu.make_async_copy(result.at[:, mine], out.at[:, mine], sems.at[blocks + k])])
    wait_all(sent)


def local_call(kernel, outs, scratch, place, *arrays, flops, out_space=pltpu.VMEM, aliases=()):
    shapes = [jax.ShapeDtypeStruct(s, jnp.bfloat16) for s in outs]
    single = len(shapes) == 1
    spec = pl.BlockSpec(memory_space=out_space)
    return pl.pallas_call(
        kernel,
        out_shape=shapes[0] if single else shapes,
        in_specs=[pl.BlockSpec(memory_space=pltpu.SMEM)] + [pl.BlockSpec(memory_space=pl.ANY)] * len(arrays),
        out_specs=spec if single else [spec] * len(shapes),
        scratch_shapes=scratch,
        input_output_aliases=dict(aliases),
        cost_estimate=pl.CostEstimate(flops=flops, bytes_accessed=4 << 20, transcendentals=0),
        compiler_params=pltpu.CompilerParams(vmem_limit_bytes=16 << 20),
    )(place, *arrays)


def body(activations, out_grads, block_mask, master_weight, first_moment, second_moment):
    nx, ny, nl = (lax.axis_size(k) for k in ("x", "y", "zl"))
    x, y, zl, core = (lax.axis_index(k) for k in ("x", "y", "zl", "core"))
    place = jnp.stack([x, y, zl, core]).astype(jnp.int32)
    rows, cols = master_weight.shape
    acts, grads = activations[0], out_grads[0]
    tok, wide = acts.shape
    held = grads.shape[0]

    mask_rows = rows // BLOCK
    keep = expand(lax.dynamic_slice_in_dim(block_mask, x * mask_rows, mask_rows, 0))

    by_zh = from_everyone(grads, "zh")
    own = master_weight.astype(jnp.bfloat16) * keep.astype(jnp.bfloat16)
    near = jnp.stack([own, swapped(own, "y", 1)])
    far = swapped(near, "y", 2)

    def cut(k):
        return lax.dynamic_slice_in_dim(acts, k * rows, rows, 1)

    here, first, second, third = (cut(k) for k in partners(x))
    arrived = swapped(jnp.stack([first, third]), "x", 1)
    crossed = swapped(jnp.stack([second, arrived[1]]), "x", 2)
    chunk = jnp.concatenate([here[None], arrived[:1], crossed])
    by_zh, chunk = lax.optimization_barrier((by_zh, chunk))

    spread = jnp.broadcast_to(by_zh, (nx, *by_zh.shape)).reshape(nx * ny, held, cols)
    mine = lax.all_to_all(spread, ("x", "y"), 0, 0, tiled=True)
    pieces = [chunk] + [shifted(chunk, "zl", s) for s in range(1, nl)]
    mine = mine.reshape(nx, ny, held, cols)
    theirs = shifted(mine, "core", 1)

    flops = 2 * nx * 2 * held * ny * cols * rows
    half_tile = (nx, held, ny * cols)
    scratch = [
        pltpu.VMEM(half_tile, jnp.bfloat16),
        pltpu.VMEM((rows, ny * cols), jnp.bfloat16),
        pltpu.VMEM((nx, 2, tok, rows), jnp.bfloat16),
        pltpu.SemaphoreType.DMA((10,)),
    ]
    shape = [(nx, 2, 2, tok, rows)]
    begun = local_call(own_half_kernel, shape, scratch, place, mine, near, far, flops=flops // 2, out_space=pl.ANY)
    part = local_call(
        other_half_kernel, shape, scratch, place, theirs, near, far, begun,
        flops=flops // 2, out_space=pl.ANY, aliases={4: 0},
    )
    parts = lax.all_to_all(part.reshape(nx * nl, tok, rows), ("x", "zl"), 0, 0, tiled=True)

    got = local_call(
        weights_kernel,
        [(rows, cols)] * ny,
        [
            pltpu.VMEM((2, *half_tile), jnp.bfloat16),
            pltpu.VMEM((2, nx, 2, tok, rows), jnp.bfloat16),
            pltpu.VMEM((rows, nx * 4 * tok), jnp.bfloat16),
            pltpu.SemaphoreType.DMA((24,)),
        ],
        place, mine, theirs, *pieces, flops=flops,
    )
    got = [got[0]] + [swapped(got[s], "y", s) for s in range(1, ny)]
    grad = keep * sum(g.astype(jnp.float32) for g in got)

    new_first = first_decay * first_moment + (1.0 - first_decay) * grad
    new_second = second_decay * second_moment + (1.0 - second_decay) * grad * grad
    step_size = new_first / first_correct / (jnp.sqrt(new_second / second_correct) + adam_epsilon)
    new_weight = keep * (master_weight - learn_rate * step_size)

    input_grads = pl.pallas_call(
        sum_kernel,
        out_shape=jax.ShapeDtypeStruct((tok, wide), jnp.bfloat16),
        in_specs=[pl.BlockSpec(memory_space=pl.ANY)],
        out_specs=pl.BlockSpec(memory_space=pl.ANY),
        scratch_shapes=[
            pltpu.VMEM((nx, nl, tok, rows), jnp.bfloat16),
            pltpu.VMEM((tok, wide), jnp.bfloat16),
            pltpu.SemaphoreType.DMA((2 * nx,)),
        ],
    )(parts.reshape(nx, nl, tok, rows))
    return (input_grads[None], new_weight, new_first, new_second)


def solution(mesh):
    finer = Mesh(mesh.devices.reshape(4, 2, 4, 4, 4), ("zh", "core", "y", "zl", "x"))
    weight_spec = P(ROW_X, COL)
    in_specs = (P("x", COL, ROW), P("x", ROW, COL), P(ROW, COL), weight_spec, weight_spec, weight_spec)
    out_specs = (P("x", COL, ROW), weight_spec, weight_spec, weight_spec)
    return jax.shard_map(body, mesh=finer, in_specs=in_specs, out_specs=out_specs, check_vma=False)
```

profile of v0, /device:TPU:32, one launch (start us, length us, event | category | flops | bytes accessed | tf_op | source)
XLA Modules:
  0.0 170.9 jit_solution(7371515494796040281)
XLA Ops:
  0.6 1.6 broadcast_in_dim.16
  2.2 14.3 %all-to-all-start = ((bf16[4,128,256]{2,1,0:T(8,128)(2,1)}), bf16[4,128,256]{2,1,0:T(8,128)(2,1)S(1)}, u32[]{:S(2)}, u32[]{:S(2)}) async-start(bf16[4,128,256]{2,1,0:T(8,128)(2,1)} %broadcast_in_dim.16), calls=%async_computation | async-start | bytes 524288 | tf_op jit(solution)/shard_map/all_to_all | solution.py:25
  16.6 3.4 %collective-permute-start = (bf16[2,64,512]{2,1,0:T(8,128)(2,1)S(1)}, bf16[2,64,512]{2,1,0:T(8,128)(2,1)S(1)}, u32[]{:S(2)}, u32[]{:S(2)}) collective-permute-start(bf16[2,64,512]{2,1,0:T(8,128)(2,1)S(1)} %pad_maximum_fusion.2), channel_id=1, source_target_pairs={{0,1},{1,0},{2,3},{3,2},{4,5},{5,4},{6,7},{7,6},{8,9},{9,8},{10,11... | collective-permute-start | bytes 393224 | tf_op jit(solution)/shard_map/ppermute | solution.py:39
  20.0 3.5 %collective-permute-done = bf16[2,64,512]{2,1,0:T(8,128)(2,1)S(1)} collective-permute-done((bf16[2,64,512]{2,1,0:T(8,128)(2,1)S(1)}, bf16[2,64,512]{2,1,0:T(8,128)(2,1)S(1)}, u32[]{:S(2)}, u32[]{:S(2)}) %collective-permute-start) | collective-permute-done | bytes 131104 | tf_op jit(solution)/shard_map/ppermute | solution.py:39
  23.5 4.7 %collective-permute-start.1 = (bf16[2,64,512]{2,1,0:T(8,128)(2,1)S(1)}, bf16[2,64,512]{2,1,0:T(8,128)(2,1)S(1)}, u32[]{:S(2)}, u32[]{:S(2)}) collective-permute-start(bf16[2,64,512]{2,1,0:T(8,128)(2,1)S(1)} %pad_maximum_fusion.3), channel_id=1, source_target_pairs={{0,3},{1,2},{2,1},{3,0},{4,7},{5,6},{6,5},{7,4},{8,11},{9,10},{10,... | collective-permute-start | bytes 393224 | tf_op jit(solution)/shard_map/ppermute | solution.py:39
  28.1 3.4 %collective-permute-done.1 = bf16[2,64,512]{2,1,0:T(8,128)(2,1)S(1)} collective-permute-done((bf16[2,64,512]{2,1,0:T(8,128)(2,1)S(1)}, bf16[2,64,512]{2,1,0:T(8,128)(2,1)S(1)}, u32[]{:S(2)}, u32[]{:S(2)}) %collective-permute-start.1) | collective-permute-done | bytes 131104 | tf_op jit(solution)/shard_map/ppermute | solution.py:39
  31.6 5.8 %all-to-all-done = bf16[4,128,256]{2,1,0:T(8,128)(2,1)S(1)} async-done(((bf16[4,128,256]{2,1,0:T(8,128)(2,1)}), bf16[4,128,256]{2,1,0:T(8,128)(2,1)S(1)}, u32[]{:S(2)}, u32[]{:S(2)}) %all-to-all-start) | async-done | bytes 262176 | tf_op jit(solution)/shard_map/all_to_all | solution.py:25
  38.5 7.2 %all-to-all-start.1 = ((bf16[16,128,256]{2,1,0:T(8,128)(2,1)}), bf16[16,128,256]{2,1,0:T(8,128)(2,1)S(1)}, u32[]{:S(2)}, u32[]{:S(2)}) async-start(bf16[16,128,256]{2,1,0:T(8,128)(2,1)} %bitcast.5), calls=%async_computation.1 | async-start | bytes 2097152 | tf_op jit(solution)/shard_map/all_to_all | solution.py:192
  45.9 15.4 %all-to-all-done.1 = bf16[16,128,256]{2,1,0:T(8,128)(2,1)S(1)} async-done(((bf16[16,128,256]{2,1,0:T(8,128)(2,1)}), bf16[16,128,256]{2,1,0:T(8,128)(2,1)S(1)}, u32[]{:S(2)}, u32[]{:S(2)}) %all-to-all-start.1) | async-done | bytes 1048608 | tf_op jit(solution)/shard_map/all_to_all | solution.py:192
  61.2 1.9 %collective-permute-start.2 = (bf16[4,4,128,256]{3,2,1,0:T(8,128)(2,1)S(1)}, bf16[4,4,128,256]{3,2,1,0:T(8,128)(2,1)S(1)}, u32[]{:S(2)}, u32[]{:S(2)}) collective-permute-start(bf16[4,4,128,256]{3,2,1,0:T(8,128)(2,1)S(1)} %bitcast.26), channel_id=1, source_target_pairs={{0,64},{64,0},{1,65},{65,1},{2,66},{66,2},{3,67},{67,3},{4,68},{68... | collective-permute-start | bytes 3145736 | tf_op jit(solution)/shard_map/ppermute | solution.py:30
  64.2 2.5 %collective-permute-start.3 = (bf16[512,256]{1,0:T(8,128)(2,1)S(1)}, bf16[512,256]{1,0:T(8,128)(2,1)S(1)}, u32[]{:S(2)}, u32[]{:S(2)}) collective-permute-start(bf16[512,256]{1,0:T(8,128)(2,1)S(1)} %fusion.1), channel_id=1, source_target_pairs={{0,16},{16,0},{32,48},{48,32},{1,17},{17,1},{33,49},{49,33},{2,18}... | collective-permute-start | bytes 786440 | tf_op jit(solution)/shard_map/ppermute | solution.py:39
  66.6 8.1 %collective-permute-done.3 = bf16[512,256]{1,0:T(8,128)(2,1)S(1)} collective-permute-done((bf16[512,256]{1,0:T(8,128)(2,1)S(1)}, bf16[512,256]{1,0:T(8,128)(2,1)S(1)}, u32[]{:S(2)}, u32[]{:S(2)}) %collective-permute-start.3) | collective-permute-done | bytes 262176 | tf_op jit(solution)/shard_map/ppermute | solution.py:39
  74.8 2.8 %collective-permute-start.4 = (bf16[2,512,256]{2,1,0:T(8,128)(2,1)S(1)}, bf16[2,512,256]{2,1,0:T(8,128)(2,1)S(1)}, u32[]{:S(2)}, u32[]{:S(2)}) collective-permute-start(bf16[2,512,256]{2,1,0:T(8,128)(2,1)S(1)} %pad_maximum_fusion.near), channel_id=1, source_target_pairs={{0,48},{16,32},{32,16},{48,0},{1,49},{17,33},{33,17},{49,1},{2,50}... | collective-permute-start | bytes 1572872 | tf_op jit(solution)/shard_map/ppermute | solution.py:39
  77.7 13.6 %collective-permute-done.4.far = bf16[2,512,256]{2,1,0:T(8,128)(2,1)S(1)} collective-permute-done((bf16[2,512,256]{2,1,0:T(8,128)(2,1)S(1)}, bf16[2,512,256]{2,1,0:T(8,128)(2,1)S(1)}, u32[]{:S(2)}, u32[]{:S(2)}) %collective-permute-start.4) | collective-permute-done | bytes 524320 | tf_op jit(solution)/shard_map/ppermute | solution.py:39
  91.4 2.4 %shard_map.93.begun = bf16[4,2,2,64,512]{4,3,2,1,0:T(8,128)(2,1)} custom-call(s32[4]{0:T(128)S(1)} %pad_add_fusion.place, bf16[4,4,128,256]{3,2,1,0:T(8,128)(2,1)S(1)} %bitcast.27, bf16[2,512,256]{2,1,0:T(8,128)(2,1)S(1)} %pad_maximum_fusion.near, bf16[2,512,256]{2,1,0:T(8,128)(2,1)S(1)} %collective-permute-done.4.far), custom_call_target="tpu_custom_call" | custom-call | flops 536870912 | bytes 4194304 | tf_op jit(solution)/shard_map/pallas_call | solution.py:153
  93.8 2.4 %shard_map.94 = bf16[4,2,2,64,512]{4,3,2,1,0:T(8,128)(2,1)} custom-call(s32[4]{0:T(128)S(1)} %pad_add_fusion.place, bf16[4,4,128,256]{3,2,1,0:T(8,128)(2,1)S(1)} %collective-permute-done.2.source.theirs, bf16[2,512,256]{2,1,0:T(8,128)(2,1)S(1)} %pad_maximum_fusion.near, ...), custom_call_target="tpu_custom_call", output_to_operand_aliasing={{}: (4, {})} | custom-call | flops 536870912 | bytes 4194304 | tf_op jit(solution)/shard_map/pallas_call | solution.py:153
  96.2 4.4 %all-to-all-start.2 = ((bf16[16,64,512]{2,1,0:T(8,128)(2,1)}), bf16[16,64,512]{2,1,0:T(8,128)(2,1)}, u32[]{:S(2)}, u32[]{:S(2)}) async-start(bf16[16,64,512]{2,1,0:T(8,128)(2,1)} %bitcast.9), calls=%async_computation.2 | async-start | bytes 2097152 | tf_op jit(solution)/shard_map/all_to_all | solution.py:211
  100.6 3.5 %collective-permute-start.5 = (bf16[4,64,512]{2,1,0:T(8,128)(2,1)S(1)}, bf16[4,64,512]{2,1,0:T(8,128)(2,1)S(1)}, u32[]{:S(2)}, u32[]{:S(2)}) collective-permute-start(bf16[4,64,512]{2,1,0:T(8,128)(2,1)S(1)} %pad_maximum_fusion.1.a0), channel_id=1, source_target_pairs={{0,4},{4,8},{8,12},{12,0},{1,5},{5,9},{9,13},{13,1},{2,6},{6,10},{... | collective-permute-start | bytes 786440 | tf_op jit(solution)/shard_map/ppermute | solution.py:30
  104.1 3.0 %collective-permute-start.6 = (bf16[4,64,512]{2,1,0:T(8,128)(2,1)S(1)}, bf16[4,64,512]{2,1,0:T(8,128)(2,1)S(1)}, u32[]{:S(2)}, u32[]{:S(2)}) collective-permute-start(bf16[4,64,512]{2,1,0:T(8,128)(2,1)S(1)} %pad_maximum_fusion.1.a0), channel_id=1, source_target_pairs={{0,8},{4,12},{8,0},{12,4},{1,9},{5,13},{9,1},{13,5},{2,10},{6,14},... | collective-permute-start | bytes 786440 | tf_op jit(solution)/shard_map/ppermute | solution.py:30
  107.1 3.8 %collective-permute-start.7 = (bf16[4,64,512]{2,1,0:T(8,128)(2,1)S(1)}, bf16[4,64,512]{2,1,0:T(8,128)(2,1)S(1)}, u32[]{:S(2)}, u32[]{:S(2)}) collective-permute-start(bf16[4,64,512]{2,1,0:T(8,128)(2,1)S(1)} %pad_maximum_fusion.1.a0), channel_id=1, source_target_pairs={{0,12},{4,0},{8,4},{12,8},{1,13},{5,1},{9,5},{13,9},{2,14},{6,2},{... | collective-permute-start | bytes 786440 | tf_op jit(solution)/shard_map/ppermute | solution.py:30
  110.9 28.0 %collective-permute-done.5.a1 = bf16[4,64,512]{2,1,0:T(8,128)(2,1)S(1)} collective-permute-done((bf16[4,64,512]{2,1,0:T(8,128)(2,1)S(1)}, bf16[4,64,512]{2,1,0:T(8,128)(2,1)S(1)}, u32[]{:S(2)}, u32[]{:S(2)}) %collective-permute-start.5) | collective-permute-done | bytes 262176 | tf_op jit(solution)/shard_map/ppermute | solution.py:30
  138.9 5.3 %collective-permute-done.6.a2 = bf16[4,64,512]{2,1,0:T(8,128)(2,1)S(1)} collective-permute-done((bf16[4,64,512]{2,1,0:T(8,128)(2,1)S(1)}, bf16[4,64,512]{2,1,0:T(8,128)(2,1)S(1)}, u32[]{:S(2)}, u32[]{:S(2)}) %collective-permute-start.6) | collective-permute-done | bytes 262176 | tf_op jit(solution)/shard_map/ppermute | solution.py:30
  144.1 2.1 %collective-permute-done.7.a3 = bf16[4,64,512]{2,1,0:T(8,128)(2,1)S(1)} collective-permute-done((bf16[4,64,512]{2,1,0:T(8,128)(2,1)S(1)}, bf16[4,64,512]{2,1,0:T(8,128)(2,1)S(1)}, u32[]{:S(2)}, u32[]{:S(2)}) %collective-permute-start.7) | collective-permute-done | bytes 262176 | tf_op jit(solution)/shard_map/ppermute | solution.py:30
  146.3 4.1 %shard_map.96 = (bf16[512,256]{1,0:T(8,128)(2,1)S(1)}, bf16[512,256]{1,0:T(8,128)(2,1)S(1)}, bf16[512,256]{1,0:T(8,128)(2,1)S(1)}, bf16[512,256]{1,0:T(8,128)(2,1)S(1)}) custom-call(s32[4]{0:T(128)S(1)} %pad_add_fusion.place, bf16[4,4,128,256]{3,2,1,0:T(8,128)(2,1)S(1)} %bitcast.28, bf16[4,4,128,256]{3,2,1,0:T(8,128)(2,1)S(1)} %collective-permute-done.2.source.theirs, ...), custom_call_target="tpu_custom_call" | custom-call | flops 1073741824 | bytes 4194304 | tf_op jit(solution)/shard_map/pallas_call | solution.py:153
  150.4 2.2 %collective-permute-start.10 = (bf16[512,256]{1,0:T(8,128)(2,1)S(1)}, bf16[512,256]{1,0:T(8,128)(2,1)S(1)}, u32[]{:S(2)}, u32[]{:S(2)}) collective-permute-start(bf16[512,256]{1,0:T(8,128)(2,1)S(1)} %get-tuple-element.15), channel_id=1, source_target_pairs={{0,32},{16,48},{32,0},{48,16},{1,33},{17,49},{33,1},{49,17},{2,34}... | collective-permute-start | bytes 786440 | tf_op jit(solution)/shard_map/ppermute | solution.py:39
  152.6 3.9 %collective-permute-start.8 = (bf16[512,256]{1,0:T(8,128)(2,1)S(1)}, bf16[512,256]{1,0:T(8,128)(2,1)S(1)}, u32[]{:S(2)}, u32[]{:S(2)}) collective-permute-start(bf16[512,256]{1,0:T(8,128)(2,1)S(1)} %get-tuple-element.13), channel_id=1, source_target_pairs={{0,16},{16,0},{32,48},{48,32},{1,17},{17,1},{33,49},{49,33},{2,18}... | collective-permute-start | bytes 786440 | tf_op jit(solution)/shard_map/ppermute | solution.py:39
  156.5 3.7 %collective-permute-start.9 = (bf16[512,256]{1,0:T(8,128)(2,1)S(1)}, bf16[512,256]{1,0:T(8,128)(2,1)S(1)}, u32[]{:S(2)}, u32[]{:S(2)}) collective-permute-start(bf16[512,256]{1,0:T(8,128)(2,1)S(1)} %get-tuple-element.14), channel_id=1, source_target_pairs={{0,48},{16,32},{32,16},{48,0},{1,49},{17,33},{33,17},{49,1},{2,50}... | collective-permute-start | bytes 786440 | tf_op jit(solution)/shard_map/ppermute | solution.py:39
  160.2 2.7 %collective-permute-done.10 = bf16[512,256]{1,0:T(8,128)(2,1)S(1)} collective-permute-done((bf16[512,256]{1,0:T(8,128)(2,1)S(1)}, bf16[512,256]{1,0:T(8,128)(2,1)S(1)}, u32[]{:S(2)}, u32[]{:S(2)}) %collective-permute-start.10) | collective-permute-done | bytes 262176 | tf_op jit(solution)/shard_map/ppermute | solution.py:39
  162.9 2.5 %collective-permute-done.8 = bf16[512,256]{1,0:T(8,128)(2,1)S(1)} collective-permute-done((bf16[512,256]{1,0:T(8,128)(2,1)S(1)}, bf16[512,256]{1,0:T(8,128)(2,1)S(1)}, u32[]{:S(2)}, u32[]{:S(2)}) %collective-permute-start.8) | collective-permute-done | bytes 262176 | tf_op jit(solution)/shard_map/ppermute | solution.py:39
  165.4 2.0 %collective-permute-done.9 = bf16[512,256]{1,0:T(8,128)(2,1)S(1)} collective-permute-done((bf16[512,256]{1,0:T(8,128)(2,1)S(1)}, bf16[512,256]{1,0:T(8,128)(2,1)S(1)}, u32[]{:S(2)}, u32[]{:S(2)}) %collective-permute-start.9) | collective-permute-done | bytes 262176 | tf_op jit(solution)/shard_map/ppermute | solution.py:39
  167.5 1.5 bitcast_multiply_fusion
  169.0 1.9 %shard_map.95 = bf16[64,2048]{1,0:T(8,128)(2,1)} custom-call(bf16[4,4,64,512]{3,2,1,0:T(8,128)(2,1)} %bitcast.10.parts), custom_call_target="tpu_custom_call" | custom-call | tf_op jit(solution)/shard_map/pallas_call | solution.py:232
  (30 shorter events, 2.5 us)
Async XLA Ops:
  2.2 14.3 %copy-start.6 = (bf16[1,64,2048]{2,1,0:T(8,128)(2,1)S(1)}, bf16[1,64,2048]{2,1,0:T(8,128)(2,1)}, u32[]{:S(2)}) copy-start(bf16[1,64,2048]{2,1,0:T(8,128)(2,1)} %param.6) | copy-start | bytes 786436
  2.2 35.2 %all-to-all-start = ((bf16[4,128,256]{2,1,0:T(8,128)(2,1)}), bf16[4,128,256]{2,1,0:T(8,128)(2,1)S(1)}, u32[]{:S(2)}, u32[]{:S(2)}) async-start(bf16[4,128,256]{2,1,0:T(8,128)(2,1)} %broadcast_in_dim.16), calls=%async_computation | async-start | bytes 524288 | tf_op jit(solution)/shard_map/all_to_all | solution.py:25
  16.6 6.9 %collective-permute-start = (bf16[2,64,512]{2,1,0:T(8,128)(2,1)S(1)}, bf16[2,64,512]{2,1,0:T(8,128)(2,1)S(1)}, u32[]{:S(2)}, u32[]{:S(2)}) collective-permute-start(bf16[2,64,512]{2,1,0:T(8,128)(2,1)S(1)} %pad_maximum_fusion.2), channel_id=1, source_target_pairs={{0,1},{1,0},{2,3},{3,2},{4,5},{5,4},{6,7},{7,6},{8,9},{9,8},{10,11... | collective-permute-start | bytes 393224 | tf_op jit(solution)/shard_map/ppermute | solution.py:39
  23.5 8.1 %collective-permute-start.1 = (bf16[2,64,512]{2,1,0:T(8,128)(2,1)S(1)}, bf16[2,64,512]{2,1,0:T(8,128)(2,1)S(1)}, u32[]{:S(2)}, u32[]{:S(2)}) collective-permute-start(bf16[2,64,512]{2,1,0:T(8,128)(2,1)S(1)} %pad_maximum_fusion.3), channel_id=1, source_target_pairs={{0,3},{1,2},{2,1},{3,0},{4,7},{5,6},{6,5},{7,4},{8,11},{9,10},{10,... | collective-permute-start | bytes 393224 | tf_op jit(solution)/shard_map/ppermute | solution.py:39
  38.5 7.2 %copy-start.7 = (s32[16,2]{0,1:T(2,128)S(1)}, s32[16,2]{0,1:T(2,128)}, u32[]{:S(2)}) copy-start(s32[16,2]{0,1:T(2,128)} %param.8) | copy-start | bytes 388
  38.5 22.7 %all-to-all-start.1 = ((bf16[16,128,256]{2,1,0:T(8,128)(2,1)}), bf16[16,128,256]{2,1,0:T(8,128)(2,1)S(1)}, u32[]{:S(2)}, u32[]{:S(2)}) async-start(bf16[16,128,256]{2,1,0:T(8,128)(2,1)} %bitcast.5), calls=%async_computation.1 | async-start | bytes 2097152 | tf_op jit(solution)/shard_map/all_to_all | solution.py:192
  45.7 17.7 %copy-start.2 = (f32[512,256]{1,0:T(8,128)S(1)}, f32[512,256]{1,0:T(8,128)}, u32[]{:S(2)}) copy-start(f32[512,256]{1,0:T(8,128)} %param.9) | copy-start | bytes 1572868
  61.2 32.5 %collective-permute-start.2 = (bf16[4,4,128,256]{3,2,1,0:T(8,128)(2,1)S(1)}, bf16[4,4,128,256]{3,2,1,0:T(8,128)(2,1)S(1)}, u32[]{:S(2)}, u32[]{:S(2)}) collective-permute-start(bf16[4,4,128,256]{3,2,1,0:T(8,128)(2,1)S(1)} %bitcast.26), channel_id=1, source_target_pairs={{0,64},{64,0},{1,65},{65,1},{2,66},{66,2},{3,67},{67,3},{4,68},{68... | collective-permute-start | bytes 3145736 | tf_op jit(solution)/shard_map/ppermute | solution.py:30
  63.4 0.8 copy-start
  64.2 10.6 %collective-permute-start.3 = (bf16[512,256]{1,0:T(8,128)(2,1)S(1)}, bf16[512,256]{1,0:T(8,128)(2,1)S(1)}, u32[]{:S(2)}, u32[]{:S(2)}) collective-permute-start(bf16[512,256]{1,0:T(8,128)(2,1)S(1)} %fusion.1), channel_id=1, source_target_pairs={{0,16},{16,0},{32,48},{48,32},{1,17},{17,1},{33,49},{49,33},{2,18}... | collective-permute-start | bytes 786440 | tf_op jit(solution)/shard_map/ppermute | solution.py:39
  74.8 16.6 %collective-permute-start.4 = (bf16[2,512,256]{2,1,0:T(8,128)(2,1)S(1)}, bf16[2,512,256]{2,1,0:T(8,128)(2,1)S(1)}, u32[]{:S(2)}, u32[]{:S(2)}) collective-permute-start(bf16[2,512,256]{2,1,0:T(8,128)(2,1)S(1)} %pad_maximum_fusion.near), channel_id=1, source_target_pairs={{0,48},{16,32},{32,16},{48,0},{1,49},{17,33},{33,17},{49,1},{2,50}... | collective-permute-start | bytes 1572872 | tf_op jit(solution)/shard_map/ppermute | solution.py:39
  96.2 72.8 %all-to-all-start.2 = ((bf16[16,64,512]{2,1,0:T(8,128)(2,1)}), bf16[16,64,512]{2,1,0:T(8,128)(2,1)}, u32[]{:S(2)}, u32[]{:S(2)}) async-start(bf16[16,64,512]{2,1,0:T(8,128)(2,1)} %bitcast.9), calls=%async_computation.2 | async-start | bytes 2097152 | tf_op jit(solution)/shard_map/all_to_all | solution.py:211
  100.6 66.9 %copy-start.1 = (f32[4,128,2,128]{3,2,1,0:T(2,128)S(1)}, f32[4,128,2,128]{3,2,1,0:T(2,128)}, u32[]{:S(2)}) copy-start(f32[4,128,2,128]{3,2,1,0:T(2,128)} %copy-done) | copy-start | bytes 1572868
  100.6 66.8 %copy-start.3 = (f32[512,256]{1,0:T(8,128)S(1)}, f32[512,256]{1,0:T(8,128)}, u32[]{:S(2)}) copy-start(f32[512,256]{1,0:T(8,128)} %param.9) | copy-start | bytes 1572868
  100.6 66.8 %copy-start.4 = (f32[512,256]{1,0:T(8,128)S(1)}, f32[512,256]{1,0:T(8,128)}, u32[]{:S(2)}) copy-start(f32[512,256]{1,0:T(8,128)} %param.10) | copy-start | bytes 1572868
  100.6 66.8 %copy-start.5 = (f32[512,256]{1,0:T(8,128)S(1)}, f32[512,256]{1,0:T(8,128)}, u32[]{:S(2)}) copy-start(f32[512,256]{1,0:T(8,128)} %param.11) | copy-start | bytes 1572868
  100.6 38.2 %collective-permute-start.5 = (bf16[4,64,512]{2,1,0:T(8,128)(2,1)S(1)}, bf16[4,64,512]{2,1,0:T(8,128)(2,1)S(1)}, u32[]{:S(2)}, u32[]{:S(2)}) collective-permute-start(bf16[4,64,512]{2,1,0:T(8,128)(2,1)S(1)} %pad_maximum_fusion.1.a0), channel_id=1, source_target_pairs={{0,4},{4,8},{8,12},{12,0},{1,5},{5,9},{9,13},{13,1},{2,6},{6,10},{... | collective-permute-start | bytes 786440 | tf_op jit(solution)/shard_map/ppermute | solution.py:30
  104.1 40.0 %collective-permute-start.6 = (bf16[4,64,512]{2,1,0:T(8,128)(2,1)S(1)}, bf16[4,64,512]{2,1,0:T(8,128)(2,1)S(1)}, u32[]{:S(2)}, u32[]{:S(2)}) collective-permute-start(bf16[4,64,512]{2,1,0:T(8,128)(2,1)S(1)} %pad_maximum_fusion.1.a0), channel_id=1, source_target_pairs={{0,8},{4,12},{8,0},{12,4},{1,9},{5,13},{9,1},{13,5},{2,10},{6,14},... | collective-permute-start | bytes 786440 | tf_op jit(solution)/shard_map/ppermute | solution.py:30
  107.1 39.2 %collective-permute-start.7 = (bf16[4,64,512]{2,1,0:T(8,128)(2,1)S(1)}, bf16[4,64,512]{2,1,0:T(8,128)(2,1)S(1)}, u32[]{:S(2)}, u32[]{:S(2)}) collective-permute-start(bf16[4,64,512]{2,1,0:T(8,128)(2,1)S(1)} %pad_maximum_fusion.1.a0), channel_id=1, source_target_pairs={{0,12},{4,0},{8,4},{12,8},{1,13},{5,1},{9,5},{13,9},{2,14},{6,2},{... | collective-permute-start | bytes 786440 | tf_op jit(solution)/shard_map/ppermute | solution.py:30
  150.4 12.6 %collective-permute-start.10 = (bf16[512,256]{1,0:T(8,128)(2,1)S(1)}, bf16[512,256]{1,0:T(8,128)(2,1)S(1)}, u32[]{:S(2)}, u32[]{:S(2)}) collective-permute-start(bf16[512,256]{1,0:T(8,128)(2,1)S(1)} %get-tuple-element.15), channel_id=1, source_target_pairs={{0,32},{16,48},{32,0},{48,16},{1,33},{17,49},{33,1},{49,17},{2,34}... | collective-permute-start | bytes 786440 | tf_op jit(solution)/shard_map/ppermute | solution.py:39
  152.6 12.9 %collective-permute-start.8 = (bf16[512,256]{1,0:T(8,128)(2,1)S(1)}, bf16[512,256]{1,0:T(8,128)(2,1)S(1)}, u32[]{:S(2)}, u32[]{:S(2)}) collective-permute-start(bf16[512,256]{1,0:T(8,128)(2,1)S(1)} %get-tuple-element.13), channel_id=1, source_target_pairs={{0,16},{16,0},{32,48},{48,32},{1,17},{17,1},{33,49},{49,33},{2,18}... | collective-permute-start | bytes 786440 | tf_op jit(solution)/shard_map/ppermute | solution.py:39
  156.5 11.0 %collective-permute-start.9 = (bf16[512,256]{1,0:T(8,128)(2,1)S(1)}, bf16[512,256]{1,0:T(8,128)(2,1)S(1)}, u32[]{:S(2)}, u32[]{:S(2)}) collective-permute-start(bf16[512,256]{1,0:T(8,128)(2,1)S(1)} %get-tuple-element.14), channel_id=1, source_target_pairs={{0,48},{16,32},{32,16},{48,0},{1,49},{17,33},{33,17},{49,1},{2,50}... | collective-permute-start | bytes 786440 | tf_op jit(solution)/shard_map/ppermute | solution.py:39
where the time goes:
time: 172 us; the launch traced here: 171 us
  waiting for transfers between devices  92.4 us (54%)
  starting transfers between devices  61.3 us (36%)
  Pallas kernels  10.8 us (6%)
  local copies, waits for them, and re-layouts  3.76 us (2%)
  other arithmetic  1.84 us (1%)
    ppermute x7, waiting for transfers between devices, swapped(): lax.ppermute(array, axis, [(k, partners(k)[which]) for k in range(4)])  35.8 us
    ppermute x4, waiting for transfers between devices, shifted(): lax.ppermute(array, axis, [(k, (k + by) % peers) for k in range(peers)])  35.4 us
    ppermute x7, starting transfers between devices, swapped(): lax.ppermute(array, axis, [(k, partners(k)[which]) for k in range(4)])  23.2 us
    all_to_all x1, waiting for transfers between devices, body(): mine = lax.all_to_all(spread, ('x', 'y'), 0, 0, tiled=True)  15.4 us
    all_to_all x1, starting transfers between devices, from_everyone(): return lax.all_to_all(copies, axis, split_axis=0, concat_axis=0, tiled=True)  14.3 us
    ppermute x4, starting transfers between devices, shifted(): lax.ppermute(array, axis, [(k, (k + by) % peers) for k in range(peers)])  12.2 us
    pallas_call x3, Pallas kernels, local_call(): pl.pallas_call(kernel, out_shape=shapes[0] if single else shapes, in_spec...  8.86 us
    all_to_all x1, starting transfers between devices, body(): mine = lax.all_to_all(spread, ('x', 'y'), 0, 0, tiled=True)  7.17 us
  transfers between devices with their start and end apart: 14, of which 12 were waited for; matrix products, arithmetic and copies ran while one was open for 1% of the time, Pallas kernels for 4%

commit v1 on v0

--- a/solution.py
+++ b/solution.py
@@ -64,7 +64,7 @@
 def gather_grads(source, tile, sems, y):
     cols = source.shape[-1]
     return [
-        pltpu.make_async_copy(source.at[:, place_y], tile.at[:, :, pl.ds(s * cols, cols)], sems.at[s])
+        pltpu.make_async_copy(source.at[place_y], tile.at[:, :, pl.ds(s * cols, cols)], sems.at[s])
         for s, place_y in enumerate(partners(y))
     ]
 
@@ -188,10 +188,10 @@
     chunk = jnp.concatenate([here[None], arrived[:1], crossed])
     by_zh, chunk = lax.optimization_barrier((by_zh, chunk))
 
-    spread = jnp.broadcast_to(by_zh, (nx, *by_zh.shape)).reshape(nx * ny, held, cols)
-    mine = lax.all_to_all(spread, ("x", "y"), 0, 0, tiled=True)
+    spread = jnp.broadcast_to(by_zh[:, None], (ny, nx, held, cols)).reshape(ny * nx, held, cols)
+    mine = lax.all_to_all(spread, ("y", "x"), 0, 0, tiled=True)
     pieces = [chunk] + [shifted(chunk, "zl", s) for s in range(1, nl)]
-    mine = mine.reshape(nx, ny, held, cols)
+    mine = mine.reshape(ny, nx, held, cols)
     theirs = shifted(mine, "core", 1)
 
     flops = 2 * nx * 2 * held * ny * cols * rows

time: 172 us -> 172 us (level)
  no operation moved by 1% of the time
where the time goes in v1:
time: 172 us; the launch traced here: 171 us
  waiting for transfers between devices  93.9 us (55%)
  starting transfers between devices  59.6 us (35%)
  Pallas kernels  10.8 us (6%)
  local copies, waits for them, and re-layouts  3.76 us (2%)
  other arithmetic  1.84 us (1%)
    ppermute x7, waiting for transfers between devices, swapped(): lax.ppermute(array, axis, [(k, partners(k)[which]) for k in range(4)])  36.5 us
    ppermute x4, waiting for transfers between devices, shifted(): lax.ppermute(array, axis, [(k, (k + by) % peers) for k in range(peers)])  35.8 us
    ppermute x7, starting transfers between devices, swapped(): lax.ppermute(array, axis, [(k, partners(k)[which]) for k in range(4)])  22.2 us
    all_to_all x1, waiting for transfers between devices, body(): mine = lax.all_to_all(spread, ('y', 'x'), 0, 0, tiled=True)  15.8 us
    all_to_all x1, starting transfers between devices, from_everyone(): return lax.all_to_all(copies, axis, split_axis=0, concat_axis=0, tiled=True)  14.3 us
    ppermute x4, starting transfers between devices, shifted(): lax.ppermute(array, axis, [(k, (k + by) % peers) for k in range(peers)])  11.6 us
    pallas_call x3, Pallas kernels, local_call(): pl.pallas_call(kernel, out_shape=shapes[0] if single else shapes, in_spec...  8.86 us
    all_to_all x1, starting transfers between devices, body(): mine = lax.all_to_all(spread, ('y', 'x'), 0, 0, tiled=True)  7.17 us
  transfers between devices with their start and end apart: 14, of which 12 were waited for; matrix products, arithmetic and copies ran while one was open for 1% of the time, Pallas kernels for 4%

profile of v1, /device:TPU:32, one launch (start us, length us, event | category | flops | bytes accessed | tf_op | source)
XLA Modules:
  0.0 170.8 jit_solution(13027756698275711604)
XLA Ops:
  0.6 1.6 broadcast_in_dim.8
  2.2 14.3 %all-to-all-start = ((bf16[4,128,256]{2,1,0:T(8,128)(2,1)}), bf16[4,128,256]{2,1,0:T(8,128)(2,1)S(1)}, u32[]{:S(2)}, u32[]{:S(2)}) async-start(bf16[4,128,256]{2,1,0:T(8,128)(2,1)} %broadcast_in_dim.8), calls=%async_computation | async-start | bytes 524288 | tf_op jit(solution)/shard_map/all_to_all | solution.py:25
  16.6 3.4 %collective-permute-start = (bf16[2,64,512]{2,1,0:T(8,128)(2,1)S(1)}, bf16[2,64,512]{2,1,0:T(8,128)(2,1)S(1)}, u32[]{:S(2)}, u32[]{:S(2)}) collective-permute-start(bf16[2,64,512]{2,1,0:T(8,128)(2,1)S(1)} %pad_maximum_fusion.2), channel_id=1, source_target_pairs={{0,1},{1,0},{2,3},{3,2},{4,5},{5,4},{6,7},{7,6},{8,9},{9,8},{10,11... | collective-permute-start | bytes 393224 | tf_op jit(solution)/shard_map/ppermute | solution.py:39
  20.0 3.5 %collective-permute-done = bf16[2,64,512]{2,1,0:T(8,128)(2,1)S(1)} collective-permute-done((bf16[2,64,512]{2,1,0:T(8,128)(2,1)S(1)}, bf16[2,64,512]{2,1,0:T(8,128)(2,1)S(1)}, u32[]{:S(2)}, u32[]{:S(2)}) %collective-permute-start) | collective-permute-done | bytes 131104 | tf_op jit(solution)/shard_map/ppermute | solution.py:39
  23.5 4.7 %collective-permute-start.1 = (bf16[2,64,512]{2,1,0:T(8,128)(2,1)S(1)}, bf16[2,64,512]{2,1,0:T(8,128)(2,1)S(1)}, u32[]{:S(2)}, u32[]{:S(2)}) collective-permute-start(bf16[2,64,512]{2,1,0:T(8,128)(2,1)S(1)} %pad_maximum_fusion.3), channel_id=1, source_target_pairs={{0,3},{1,2},{2,1},{3,0},{4,7},{5,6},{6,5},{7,4},{8,11},{9,10},{10,... | collective-permute-start | bytes 393224 | tf_op jit(solution)/shard_map/ppermute | solution.py:39
  28.1 3.4 %collective-permute-done.1 = bf16[2,64,512]{2,1,0:T(8,128)(2,1)S(1)} collective-permute-done((bf16[2,64,512]{2,1,0:T(8,128)(2,1)S(1)}, bf16[2,64,512]{2,1,0:T(8,128)(2,1)S(1)}, u32[]{:S(2)}, u32[]{:S(2)}) %collective-permute-start.1) | collective-permute-done | bytes 131104 | tf_op jit(solution)/shard_map/ppermute | solution.py:39
  31.6 5.8 %all-to-all-done = bf16[4,128,256]{2,1,0:T(8,128)(2,1)S(1)} async-done(((bf16[4,128,256]{2,1,0:T(8,128)(2,1)}), bf16[4,128,256]{2,1,0:T(8,128)(2,1)S(1)}, u32[]{:S(2)}, u32[]{:S(2)}) %all-to-all-start) | async-done | bytes 262176 | tf_op jit(solution)/shard_map/all_to_all | solution.py:25
  38.5 7.2 %all-to-all-start.1 = ((bf16[16,128,256]{2,1,0:T(8,128)(2,1)}), bf16[16,128,256]{2,1,0:T(8,128)(2,1)S(1)}, u32[]{:S(2)}, u32[]{:S(2)}) async-start(bf16[16,128,256]{2,1,0:T(8,128)(2,1)} %bitcast.5), calls=%async_computation.1 | async-start | bytes 2097152 | tf_op jit(solution)/shard_map/all_to_all | solution.py:192
  45.9 15.8 %all-to-all-done.1 = bf16[16,128,256]{2,1,0:T(8,128)(2,1)S(1)} async-done(((bf16[16,128,256]{2,1,0:T(8,128)(2,1)}), bf16[16,128,256]{2,1,0:T(8,128)(2,1)S(1)}, u32[]{:S(2)}, u32[]{:S(2)}) %all-to-all-start.1) | async-done | bytes 1048608 | tf_op jit(solution)/shard_map/all_to_all | solution.py:192
  61.7 1.9 %collective-permute-start.2 = (bf16[4,4,128,256]{3,2,1,0:T(8,128)(2,1)S(1)}, bf16[4,4,128,256]{3,2,1,0:T(8,128)(2,1)S(1)}, u32[]{:S(2)}, u32[]{:S(2)}) collective-permute-start(bf16[4,4,128,256]{3,2,1,0:T(8,128)(2,1)S(1)} %bitcast.26), channel_id=1, source_target_pairs={{0,64},{64,0},{1,65},{65,1},{2,66},{66,2},{3,67},{67,3},{4,68},{68... | collective-permute-start | bytes 3145736 | tf_op jit(solution)/shard_map/ppermute | solution.py:30
  64.6 1.9 %collective-permute-start.3 = (bf16[512,256]{1,0:T(8,128)(2,1)S(1)}, bf16[512,256]{1,0:T(8,128)(2,1)S(1)}, u32[]{:S(2)}, u32[]{:S(2)}) collective-permute-start(bf16[512,256]{1,0:T(8,128)(2,1)S(1)} %fusion.1), channel_id=1, source_target_pairs={{0,16},{16,0},{32,48},{48,32},{1,17},{17,1},{33,49},{49,33},{2,18}... | collective-permute-start | bytes 786440 | tf_op jit(solution)/shard_map/ppermute | solution.py:39
  66.5 8.7 %collective-permute-done.3 = bf16[512,256]{1,0:T(8,128)(2,1)S(1)} collective-permute-done((bf16[512,256]{1,0:T(8,128)(2,1)S(1)}, bf16[512,256]{1,0:T(8,128)(2,1)S(1)}, u32[]{:S(2)}, u32[]{:S(2)}) %collective-permute-start.3) | collective-permute-done | bytes 262176 | tf_op jit(solution)/shard_map/ppermute | solution.py:39
  75.2 2.4 %collective-permute-start.4 = (bf16[2,512,256]{2,1,0:T(8,128)(2,1)S(1)}, bf16[2,512,256]{2,1,0:T(8,128)(2,1)S(1)}, u32[]{:S(2)}, u32[]{:S(2)}) collective-permute-start(bf16[2,512,256]{2,1,0:T(8,128)(2,1)S(1)} %pad_maximum_fusion.near), channel_id=1, source_target_pairs={{0,48},{16,32},{32,16},{48,0},{1,49},{17,33},{33,17},{49,1},{2,50}... | collective-permute-start | bytes 1572872 | tf_op jit(solution)/shard_map/ppermute | solution.py:39
  77.7 14.1 %collective-permute-done.4.far = bf16[2,512,256]{2,1,0:T(8,128)(2,1)S(1)} collective-permute-done((bf16[2,512,256]{2,1,0:T(8,128)(2,1)S(1)}, bf16[2,512,256]{2,1,0:T(8,128)(2,1)S(1)}, u32[]{:S(2)}, u32[]{:S(2)}) %collective-permute-start.4) | collective-permute-done | bytes 524320 | tf_op jit(solution)/shard_map/ppermute | solution.py:39
  91.8 2.4 %shard_map.93.begun = bf16[4,2,2,64,512]{4,3,2,1,0:T(8,128)(2,1)} custom-call(s32[4]{0:T(128)S(1)} %pad_add_fusion.place, bf16[4,4,128,256]{3,2,1,0:T(8,128)(2,1)S(1)} %bitcast.27, bf16[2,512,256]{2,1,0:T(8,128)(2,1)S(1)} %pad_maximum_fusion.near, bf16[2,512,256]{2,1,0:T(8,128)(2,1)S(1)} %collective-permute-done.4.far), custom_call_target="tpu_custom_call" | custom-call | flops 536870912 | bytes 4194304 | tf_op jit(solution)/shard_map/pallas_call | solution.py:153
  94.2 2.4 %shard_map.94 = bf16[4,2,2,64,512]{4,3,2,1,0:T(8,128)(2,1)} custom-call(s32[4]{0:T(128)S(1)} %pad_add_fusion.place, bf16[4,4,128,256]{3,2,1,0:T(8,128)(2,1)S(1)} %collective-permute-done.2.source.theirs, bf16[2,512,256]{2,1,0:T(8,128)(2,1)S(1)} %pad_maximum_fusion.near, ...), custom_call_target="tpu_custom_call", output_to_operand_aliasing={{}: (4, {})} | custom-call | flops 536870912 | bytes 4194304 | tf_op jit(solution)/shard_map/pallas_call | solution.py:153
  96.6 4.3 %all-to-all-start.2 = ((bf16[16,64,512]{2,1,0:T(8,128)(2,1)}), bf16[16,64,512]{2,1,0:T(8,128)(2,1)}, u32[]{:S(2)}, u32[]{:S(2)}) async-start(bf16[16,64,512]{2,1,0:T(8,128)(2,1)} %bitcast.9), calls=%async_computation.2 | async-start | bytes 2097152 | tf_op jit(solution)/shard_map/all_to_all | solution.py:211
  100.9 3.0 %collective-permute-start.5 = (bf16[4,64,512]{2,1,0:T(8,128)(2,1)S(1)}, bf16[4,64,512]{2,1,0:T(8,128)(2,1)S(1)}, u32[]{:S(2)}, u32[]{:S(2)}) collective-permute-start(bf16[4,64,512]{2,1,0:T(8,128)(2,1)S(1)} %pad_maximum_fusion.1.a0), channel_id=1, source_target_pairs={{0,4},{4,8},{8,12},{12,0},{1,5},{5,9},{9,13},{13,1},{2,6},{6,10},{... | collective-permute-start | bytes 786440 | tf_op jit(solution)/shard_map/ppermute | solution.py:30
  103.9 2.9 %collective-permute-start.6 = (bf16[4,64,512]{2,1,0:T(8,128)(2,1)S(1)}, bf16[4,64,512]{2,1,0:T(8,128)(2,1)S(1)}, u32[]{:S(2)}, u32[]{:S(2)}) collective-permute-start(bf16[4,64,512]{2,1,0:T(8,128)(2,1)S(1)} %pad_maximum_fusion.1.a0), channel_id=1, source_target_pairs={{0,8},{4,12},{8,0},{12,4},{1,9},{5,13},{9,1},{13,5},{2,10},{6,14},... | collective-permute-start | bytes 786440 | tf_op jit(solution)/shard_map/ppermute | solution.py:30
  106.9 3.8 %collective-permute-start.7 = (bf16[4,64,512]{2,1,0:T(8,128)(2,1)S(1)}, bf16[4,64,512]{2,1,0:T(8,128)(2,1)S(1)}, u32[]{:S(2)}, u32[]{:S(2)}) collective-permute-start(bf16[4,64,512]{2,1,0:T(8,128)(2,1)S(1)} %pad_maximum_fusion.1.a0), channel_id=1, source_target_pairs={{0,12},{4,0},{8,4},{12,8},{1,13},{5,1},{9,5},{13,9},{2,14},{6,2},{... | collective-permute-start | bytes 786440 | tf_op jit(solution)/shard_map/ppermute | solution.py:30
  110.6 28.1 %collective-permute-done.5.a1 = bf16[4,64,512]{2,1,0:T(8,128)(2,1)S(1)} collective-permute-done((bf16[4,64,512]{2,1,0:T(8,128)(2,1)S(1)}, bf16[4,64,512]{2,1,0:T(8,128)(2,1)S(1)}, u32[]{:S(2)}, u32[]{:S(2)}) %collective-permute-start.5) | collective-permute-done | bytes 262176 | tf_op jit(solution)/shard_map/ppermute | solution.py:30
  138.7 5.1 %collective-permute-done.6.a2 = bf16[4,64,512]{2,1,0:T(8,128)(2,1)S(1)} collective-permute-done((bf16[4,64,512]{2,1,0:T(8,128)(2,1)S(1)}, bf16[4,64,512]{2,1,0:T(8,128)(2,1)S(1)}, u32[]{:S(2)}, u32[]{:S(2)}) %collective-permute-start.6) | collective-permute-done | bytes 262176 | tf_op jit(solution)/shard_map/ppermute | solution.py:30
  143.8 2.6 %collective-permute-done.7.a3 = bf16[4,64,512]{2,1,0:T(8,128)(2,1)S(1)} collective-permute-done((bf16[4,64,512]{2,1,0:T(8,128)(2,1)S(1)}, bf16[4,64,512]{2,1,0:T(8,128)(2,1)S(1)}, u32[]{:S(2)}, u32[]{:S(2)}) %collective-permute-start.7) | collective-permute-done | bytes 262176 | tf_op jit(solution)/shard_map/ppermute | solution.py:30
  146.5 4.1 %shard_map.96 = (bf16[512,256]{1,0:T(8,128)(2,1)S(1)}, bf16[512,256]{1,0:T(8,128)(2,1)S(1)}, bf16[512,256]{1,0:T(8,128)(2,1)S(1)}, bf16[512,256]{1,0:T(8,128)(2,1)S(1)}) custom-call(s32[4]{0:T(128)S(1)} %pad_add_fusion.place, bf16[4,4,128,256]{3,2,1,0:T(8,128)(2,1)S(1)} %bitcast.28, bf16[4,4,128,256]{3,2,1,0:T(8,128)(2,1)S(1)} %collective-permute-done.2.source.theirs, ...), custom_call_target="tpu_custom_call" | custom-call | flops 1073741824 | bytes 4194304 | tf_op jit(solution)/shard_map/pallas_call | solution.py:153
  150.5 2.0 %collective-permute-start.10 = (bf16[512,256]{1,0:T(8,128)(2,1)S(1)}, bf16[512,256]{1,0:T(8,128)(2,1)S(1)}, u32[]{:S(2)}, u32[]{:S(2)}) collective-permute-start(bf16[512,256]{1,0:T(8,128)(2,1)S(1)} %get-tuple-element.15), channel_id=1, source_target_pairs={{0,32},{16,48},{32,0},{48,16},{1,33},{17,49},{33,1},{49,17},{2,34}... | collective-permute-start | bytes 786440 | tf_op jit(solution)/shard_map/ppermute | solution.py:39
  152.5 3.5 %collective-permute-start.8 = (bf16[512,256]{1,0:T(8,128)(2,1)S(1)}, bf16[512,256]{1,0:T(8,128)(2,1)S(1)}, u32[]{:S(2)}, u32[]{:S(2)}) collective-permute-start(bf16[512,256]{1,0:T(8,128)(2,1)S(1)} %get-tuple-element.13), channel_id=1, source_target_pairs={{0,16},{16,0},{32,48},{48,32},{1,17},{17,1},{33,49},{49,33},{2,18}... | collective-permute-start | bytes 786440 | tf_op jit(solution)/shard_map/ppermute | solution.py:39
  156.0 4.3 %collective-permute-start.9 = (bf16[512,256]{1,0:T(8,128)(2,1)S(1)}, bf16[512,256]{1,0:T(8,128)(2,1)S(1)}, u32[]{:S(2)}, u32[]{:S(2)}) collective-permute-start(bf16[512,256]{1,0:T(8,128)(2,1)S(1)} %get-tuple-element.14), channel_id=1, source_target_pairs={{0,48},{16,32},{32,16},{48,0},{1,49},{17,33},{33,17},{49,1},{2,50}... | collective-permute-start | bytes 786440 | tf_op jit(solution)/shard_map/ppermute | solution.py:39
  160.4 2.7 %collective-permute-done.10 = bf16[512,256]{1,0:T(8,128)(2,1)S(1)} collective-permute-done((bf16[512,256]{1,0:T(8,128)(2,1)S(1)}, bf16[512,256]{1,0:T(8,128)(2,1)S(1)}, u32[]{:S(2)}, u32[]{:S(2)}) %collective-permute-start.10) | collective-permute-done | bytes 262176 | tf_op jit(solution)/shard_map/ppermute | solution.py:39
  163.1 1.9 %collective-permute-done.8 = bf16[512,256]{1,0:T(8,128)(2,1)S(1)} collective-permute-done((bf16[512,256]{1,0:T(8,128)(2,1)S(1)}, bf16[512,256]{1,0:T(8,128)(2,1)S(1)}, u32[]{:S(2)}, u32[]{:S(2)}) %collective-permute-start.8) | collective-permute-done | bytes 262176 | tf_op jit(solution)/shard_map/ppermute | solution.py:39
  165.0 2.3 %collective-permute-done.9 = bf16[512,256]{1,0:T(8,128)(2,1)S(1)} collective-permute-done((bf16[512,256]{1,0:T(8,128)(2,1)S(1)}, bf16[512,256]{1,0:T(8,128)(2,1)S(1)}, u32[]{:S(2)}, u32[]{:S(2)}) %collective-permute-start.9) | collective-permute-done | bytes 262176 | tf_op jit(solution)/shard_map/ppermute | solution.py:39
  167.3 1.5 bitcast_multiply_fusion
  168.9 1.9 %shard_map.95 = bf16[64,2048]{1,0:T(8,128)(2,1)} custom-call(bf16[4,4,64,512]{3,2,1,0:T(8,128)(2,1)} %bitcast.10.parts), custom_call_target="tpu_custom_call" | custom-call | tf_op jit(solution)/shard_map/pallas_call | solution.py:232
  (30 shorter events, 2.5 us)
Async XLA Ops:
  2.2 14.3 %copy-start.6 = (bf16[1,64,2048]{2,1,0:T(8,128)(2,1)S(1)}, bf16[1,64,2048]{2,1,0:T(8,128)(2,1)}, u32[]{:S(2)}) copy-start(bf16[1,64,2048]{2,1,0:T(8,128)(2,1)} %param.6) | copy-start | bytes 786436
  2.2 35.2 %all-to-all-start = ((bf16[4,128,256]{2,1,0:T(8,128)(2,1)}), bf16[4,128,256]{2,1,0:T(8,128)(2,1)S(1)}, u32[]{:S(2)}, u32[]{:S(2)}) async-start(bf16[4,128,256]{2,1,0:T(8,128)(2,1)} %broadcast_in_dim.8), calls=%async_computation | async-start | bytes 524288 | tf_op jit(solution)/shard_map/all_to_all | solution.py:25
  16.6 6.9 %collective-permute-start = (bf16[2,64,512]{2,1,0:T(8,128)(2,1)S(1)}, bf16[2,64,512]{2,1,0:T(8,128)(2,1)S(1)}, u32[]{:S(2)}, u32[]{:S(2)}) collective-permute-start(bf16[2,64,512]{2,1,0:T(8,128)(2,1)S(1)} %pad_maximum_fusion.2), channel_id=1, source_target_pairs={{0,1},{1,0},{2,3},{3,2},{4,5},{5,4},{6,7},{7,6},{8,9},{9,8},{10,11... | collective-permute-start | bytes 393224 | tf_op jit(solution)/shard_map/ppermute | solution.py:39
  23.5 8.1 %collective-permute-start.1 = (bf16[2,64,512]{2,1,0:T(8,128)(2,1)S(1)}, bf16[2,64,512]{2,1,0:T(8,128)(2,1)S(1)}, u32[]{:S(2)}, u32[]{:S(2)}) collective-permute-start(bf16[2,64,512]{2,1,0:T(8,128)(2,1)S(1)} %pad_maximum_fusion.3), channel_id=1, source_target_pairs={{0,3},{1,2},{2,1},{3,0},{4,7},{5,6},{6,5},{7,4},{8,11},{9,10},{10,... | collective-permute-start | bytes 393224 | tf_op jit(solution)/shard_map/ppermute | solution.py:39
  38.5 7.2 %copy-start.7 = (s32[16,2]{0,1:T(2,128)S(1)}, s32[16,2]{0,1:T(2,128)}, u32[]{:S(2)}) copy-start(s32[16,2]{0,1:T(2,128)} %param.8) | copy-start | bytes 388
  38.5 23.2 %all-to-all-start.1 = ((bf16[16,128,256]{2,1,0:T(8,128)(2,1)}), bf16[16,128,256]{2,1,0:T(8,128)(2,1)S(1)}, u32[]{:S(2)}, u32[]{:S(2)}) async-start(bf16[16,128,256]{2,1,0:T(8,128)(2,1)} %bitcast.5), calls=%async_computation.1 | async-start | bytes 2097152 | tf_op jit(solution)/shard_map/all_to_all | solution.py:192
  45.7 18.1 %copy-start.2 = (f32[512,256]{1,0:T(8,128)S(1)}, f32[512,256]{1,0:T(8,128)}, u32[]{:S(2)}) copy-start(f32[512,256]{1,0:T(8,128)} %param.9) | copy-start | bytes 1572868
  61.7 32.5 %collective-permute-start.2 = (bf16[4,4,128,256]{3,2,1,0:T(8,128)(2,1)S(1)}, bf16[4,4,128,256]{3,2,1,0:T(8,128)(2,1)S(1)}, u32[]{:S(2)}, u32[]{:S(2)}) collective-permute-start(bf16[4,4,128,256]{3,2,1,0:T(8,128)(2,1)S(1)} %bitcast.26), channel_id=1, source_target_pairs={{0,64},{64,0},{1,65},{65,1},{2,66},{66,2},{3,67},{67,3},{4,68},{68... | collective-permute-start | bytes 3145736 | tf_op jit(solution)/shard_map/ppermute | solution.py:30
  63.8 0.8 copy-start
  64.6 10.6 %collective-permute-start.3 = (bf16[512,256]{1,0:T(8,128)(2,1)S(1)}, bf16[512,256]{1,0:T(8,128)(2,1)S(1)}, u32[]{:S(2)}, u32[]{:S(2)}) collective-permute-start(bf16[512,256]{1,0:T(8,128)(2,1)S(1)} %fusion.1), channel_id=1, source_target_pairs={{0,16},{16,0},{32,48},{48,32},{1,17},{17,1},{33,49},{49,33},{2,18}... | collective-permute-start | bytes 786440 | tf_op jit(solution)/shard_map/ppermute | solution.py:39
  75.2 16.6 %collective-permute-start.4 = (bf16[2,512,256]{2,1,0:T(8,128)(2,1)S(1)}, bf16[2,512,256]{2,1,0:T(8,128)(2,1)S(1)}, u32[]{:S(2)}, u32[]{:S(2)}) collective-permute-start(bf16[2,512,256]{2,1,0:T(8,128)(2,1)S(1)} %pad_maximum_fusion.near), channel_id=1, source_target_pairs={{0,48},{16,32},{32,16},{48,0},{1,49},{17,33},{33,17},{49,1},{2,50}... | collective-permute-start | bytes 1572872 | tf_op jit(solution)/shard_map/ppermute | solution.py:39
  96.6 72.3 %all-to-all-start.2 = ((bf16[16,64,512]{2,1,0:T(8,128)(2,1)}), bf16[16,64,512]{2,1,0:T(8,128)(2,1)}, u32[]{:S(2)}, u32[]{:S(2)}) async-start(bf16[16,64,512]{2,1,0:T(8,128)(2,1)} %bitcast.9), calls=%async_computation.2 | async-start | bytes 2097152 | tf_op jit(solution)/shard_map/all_to_all | solution.py:211
  100.9 66.5 %copy-start.1 = (f32[4,128,2,128]{3,2,1,0:T(2,128)S(1)}, f32[4,128,2,128]{3,2,1,0:T(2,128)}, u32[]{:S(2)}) copy-start(f32[4,128,2,128]{3,2,1,0:T(2,128)} %copy-done) | copy-start | bytes 1572868
  100.9 66.4 %copy-start.3 = (f32[512,256]{1,0:T(8,128)S(1)}, f32[512,256]{1,0:T(8,128)}, u32[]{:S(2)}) copy-start(f32[512,256]{1,0:T(8,128)} %param.9) | copy-start | bytes 1572868
  100.9 66.4 %copy-start.4 = (f32[512,256]{1,0:T(8,128)S(1)}, f32[512,256]{1,0:T(8,128)}, u32[]{:S(2)}) copy-start(f32[512,256]{1,0:T(8,128)} %param.10) | copy-start | bytes 1572868
  100.9 66.4 %copy-start.5 = (f32[512,256]{1,0:T(8,128)S(1)}, f32[512,256]{1,0:T(8,128)}, u32[]{:S(2)}) copy-start(f32[512,256]{1,0:T(8,128)} %param.11) | copy-start | bytes 1572868
  100.9 37.8 %collective-permute-start.5 = (bf16[4,64,512]{2,1,0:T(8,128)(2,1)S(1)}, bf16[4,64,512]{2,1,0:T(8,128)(2,1)S(1)}, u32[]{:S(2)}, u32[]{:S(2)}) collective-permute-start(bf16[4,64,512]{2,1,0:T(8,128)(2,1)S(1)} %pad_maximum_fusion.1.a0), channel_id=1, source_target_pairs={{0,4},{4,8},{8,12},{12,0},{1,5},{5,9},{9,13},{13,1},{2,6},{6,10},{... | collective-permute-start | bytes 786440 | tf_op jit(solution)/shard_map/ppermute | solution.py:30
  103.9 39.9 %collective-permute-start.6 = (bf16[4,64,512]{2,1,0:T(8,128)(2,1)S(1)}, bf16[4,64,512]{2,1,0:T(8,128)(2,1)S(1)}, u32[]{:S(2)}, u32[]{:S(2)}) collective-permute-start(bf16[4,64,512]{2,1,0:T(8,128)(2,1)S(1)} %pad_maximum_fusion.1.a0), channel_id=1, source_target_pairs={{0,8},{4,12},{8,0},{12,4},{1,9},{5,13},{9,1},{13,5},{2,10},{6,14},... | collective-permute-start | bytes 786440 | tf_op jit(solution)/shard_map/ppermute | solution.py:30
  106.9 39.6 %collective-permute-start.7 = (bf16[4,64,512]{2,1,0:T(8,128)(2,1)S(1)}, bf16[4,64,512]{2,1,0:T(8,128)(2,1)S(1)}, u32[]{:S(2)}, u32[]{:S(2)}) collective-permute-start(bf16[4,64,512]{2,1,0:T(8,128)(2,1)S(1)} %pad_maximum_fusion.1.a0), channel_id=1, source_target_pairs={{0,12},{4,0},{8,4},{12,8},{1,13},{5,1},{9,5},{13,9},{2,14},{6,2},{... | collective-permute-start | bytes 786440 | tf_op jit(solution)/shard_map/ppermute | solution.py:30
  150.5 12.6 %collective-permute-start.10 = (bf16[512,256]{1,0:T(8,128)(2,1)S(1)}, bf16[512,256]{1,0:T(8,128)(2,1)S(1)}, u32[]{:S(2)}, u32[]{:S(2)}) collective-permute-start(bf16[512,256]{1,0:T(8,128)(2,1)S(1)} %get-tuple-element.15), channel_id=1, source_target_pairs={{0,32},{16,48},{32,0},{48,16},{1,33},{17,49},{33,1},{49,17},{2,34}... | collective-permute-start | bytes 786440 | tf_op jit(solution)/shard_map/ppermute | solution.py:39
  152.5 12.5 %collective-permute-start.8 = (bf16[512,256]{1,0:T(8,128)(2,1)S(1)}, bf16[512,256]{1,0:T(8,128)(2,1)S(1)}, u32[]{:S(2)}, u32[]{:S(2)}) collective-permute-start(bf16[512,256]{1,0:T(8,128)(2,1)S(1)} %get-tuple-element.13), channel_id=1, source_target_pairs={{0,16},{16,0},{32,48},{48,32},{1,17},{17,1},{33,49},{49,33},{2,18}... | collective-permute-start | bytes 786440 | tf_op jit(solution)/shard_map/ppermute | solution.py:39
  156.0 11.3 %collective-permute-start.9 = (bf16[512,256]{1,0:T(8,128)(2,1)S(1)}, bf16[512,256]{1,0:T(8,128)(2,1)S(1)}, u32[]{:S(2)}, u32[]{:S(2)}) collective-permute-start(bf16[512,256]{1,0:T(8,128)(2,1)S(1)} %get-tuple-element.14), channel_id=1, source_target_pairs={{0,48},{16,32},{32,16},{48,0},{1,49},{17,33},{33,17},{49,1},{2,50}... | collective-permute-start | bytes 786440 | tf_op jit(solution)/shard_map/ppermute | solution.py:39
